TPU v7x, 256 devices: a whole 4x4x8 slice. The times are simulated.
256 devices in a mesh: tp: 8 (over z), dp: 4 (over y), pp: 8 (over x, core).
Axes of the slice: x: 4, y: 4, z: 8, core: 2. Of those that a mesh axis runs over, the one named last changes fastest.
Arguments:
- master: float32 [50304, 1024], P('tp')
- exp_avg: float32 [50304, 1024], P('tp')
- exp_avg_sq: float32 [50304, 1024], P('tp')
- stage_ids: int32 [8, 24, 256], P('pp', 'dp')
- stage_acts: bfloat16 [8, 24, 256, 1024], P('pp', 'dp')
Outputs:
- output 1: float32 [50304, 1024], P('tp')
- output 2: float32 [50304, 1024], P('tp')
- output 3: float32 [50304, 1024], P('tp')
- output 4: bfloat16 [50304, 1024], P('tp')
All inputs are finite; a program needn't handle non-finite values.
Results may differ from a plain program's by a relative error of at most 0.001.
Values sent between devices are 32-bit elements.
A program may use at most 768 MiB of HBM per device.

v0:
```python
import functools

import jax
import jax.numpy as jnp
from jax import lax
from jax.experimental import pallas as pl
from jax.experimental.pallas import tpu as pltpu
from jax.sharding import PartitionSpec as P

LEARN_RATE = 0.003
BETA_ONE = 0.9
BETA_TWO = 0.95
ADAM_EPS = 1e-8
WEIGHT_DECAY = 0.1
CLIP_NORM = 1.0
OPT_STEP = 10

MESH_ID = pl.DeviceIdType.MESH
LOW = -1e30
VMEM = pltpu.VMEM
DMA = pltpu.SemaphoreType.DMA
F32, BF16 = jnp.float32, jnp.bfloat16
SMALL_GRANT = 21 << 19
scope = jax.named_scope


def remote(src, dst, send, recv, where):
    return pltpu.make_async_remote_copy(src_ref=src, dst_ref=dst, send_sem=send, recv_sem=recv, device_id=where, device_id_type=MESH_ID)


def in_vmem(arr):
    return pltpu.with_memory_space_constraint(arr, VMEM)


def enter(groups):
    barrier = pltpu.get_barrier_semaphore()
    for axis, peer in groups:
        pl.semaphore_signal(barrier, inc=1, device_id={axis: peer}, device_id_type=MESH_ID)
    pl.semaphore_wait(barrier, len(groups))


def ring_plan(n_one, n_two):
    items = [(1, s, 0) for s in range(n_one - 1)] + [(2, s, t) for s in range(n_one) for t in range(n_two - 1)]
    return sorted(items, key=lambda i: (i[1] + i[2], i[0], i[2]))


def grad_kernel(n_tp, n_dp, n_pp, n_chunk, lag, table_ref, acts_ref, ids_ref, sq_ref, g_ref, scale_ref, big_ref, hid_ref, dx_ref, lab_ref, look_ref, tab_ref, dl_ref, stat_ref, mid_ref, buf_p, buf_z, nb_p, nb_y, nb_z, load_s, feed_s, send_x, send_z, send_d, send_e, recv_x, recv_z, recv_d, recv_e, id_s, id_r, sp_s, sp_r, sz_s, sz_r, rs_s, rs_r, np_s, np_r, ny_s, ny_r, nz_s, nz_r, ag_s, ag_r, d_s, d_r, pre_s):
    p, z, y = lax.axis_index("pp"), lax.axis_index("tp"), lax.axis_index("dp")
    n_x = n_pp // 2
    x, c, par = p // 2, lax.rem(p, 2), lax.rem(z, 2)
    mate = 2 * x + 1 - c
    vocab = table_ref.shape[0]
    rows, tok = dl_ref.shape
    dq = g_ref.shape[3]
    up_y, down_y = lax.rem(y + 1, n_dp), lax.rem(y + n_dp - 1, n_dp)

    def first_row(d):
        return (d * n_pp + p) * rows

    n_piece, n_group = 6, 3
    wide = tok // n_piece
    per_band = min(n_piece, table_ref.shape[1] // wide)
    exp_row = 2 * tok
    part_row = exp_row + -(-n_piece // per_band) * n_dp * rows
    rel_row, one_row, com_row = (part_row + (n_dp + i) * rows for i in range(3))

    def exp_at(g, d, count=1):
        return big_ref.at[pl.ds(exp_row + (g // per_band) * n_dp * rows + d * rows, rows), pl.ds((g % per_band) * wide, count * wide)]

    def part_at(d, q, count=1):
        return big_ref.at[pl.ds(pl.multiple_of(part_row + d * rows, 8), rows), pl.ds(q * dq, count * dq)]

    def half_at(row, half):
        return big_ref.at[pl.ds(row, rows), pl.ds(2 * half * dq, 2 * dq)]

    short = vocab - (n_dp * n_pp - 1) * rows

    def table_copies(count, blocks):
        return [pltpu.make_async_copy(table_ref.at[pl.ds(pl.multiple_of(first_row(d), 8), count)], big_ref.at[pl.ds(part_row + d * rows, count)], load_s.at[1 + d]) for d in blocks]

    def each_table_copy(act):
        for cp in table_copies(rows, range(n_dp - 1)):
            act(cp)
        for cond, count in ((p < n_pp - 1, rows), (p == n_pp - 1, short)):
            @pl.when(cond)
            def _(count=count):
                for cp in table_copies(count, (n_dp - 1,)):
                    act(cp)

    each_table_copy(lambda cp: cp.start())
    hid_buf, dx_buf = big_ref.at[pl.ds(0, tok)], big_ref.at[pl.ds(tok, tok)]
    sources = ((n_pp - 1, hid_buf, hid_ref, lab_ref), (0, dx_buf, dx_ref, look_ref))
    for source, _, low, _ in sources:
        @pl.when(p == source)
        def _(low=low):
            pltpu.make_async_copy(acts_ref, low, load_s.at[0]).start()

    enter([("pp", lax.rem(p + o, n_pp)) for o in range(1, n_pp)] + [("tp", lax.rem(z + o, n_tp)) for o in range(1, n_tp)] + [("dp", lax.rem(y + o, n_dp)) for o in range(1, n_dp)])

    step_x = 1 - 2 * c
    next_p = 2 * lax.rem(x + step_x + n_x, n_x) + c
    next_z = lax.rem(z + step_x + n_tp, n_tp)
    size = tok // (4 * n_chunk)
    last = n_chunk + lag
    per_group = n_chunk // n_group
    group = tok // n_group

    def span(core, parity, k):
        return pl.ds(pl.multiple_of((4 * k + 2 * parity + core) * size, 8), size)

    class Stream:
        def __init__(self, a):
            self.a = a
            self.source, self.buf, self.low, self.ids = sources[a]
            self.is_src = p == self.source
            s_x = self.source // 2
            self.dist = lax.rem(jnp.where(c == 0, x - s_x, s_x - x) + n_x, n_x)

        def hop(self, part, send, recv, where):
            return remote(self.buf.at[part], self.buf.at[part], send, recv, where)

        def feed(self, k):
            return self.hop(span(1 - c, par, k), feed_s.at[self.a, k], recv_x.at[self.a, k], {"pp": mate})

        def ring(self, k):
            return self.hop(span(c, par, k), send_x.at[self.a, k], recv_x.at[self.a, k], {"pp": next_p})

        def plane(self, k, parity):
            return self.hop(span(c, parity, k), send_z.at[self.a, k], recv_z.at[self.a, k], {"tp": next_z})

        def across(self, k, core):
            return self.hop(span(core, par, k), send_d.at[self.a, k], recv_d.at[self.a, k], {"pp": mate})

        def again(self, k, core):
            return self.hop(span(core, 1 - par, k), send_e.at[self.a, k], recv_e.at[self.a, k], {"pp": mate})

        def id_copy(self, o):
            return remote(ids_ref, self.ids, id_s.at[self.a, o - 1], id_r.at[self.a], {"pp": lax.rem(p + o, n_pp)})

        def begin(self, with_ring):
            @pl.when(self.is_src)
            def _():
                pltpu.make_async_copy(acts_ref, self.low, load_s.at[0]).wait()
                self.ids[...] = ids_ref[...]

                @pl.loop(0, n_chunk)
                def _(k):
                    def widen(part):
                        self.buf[part, :] = self.low[part, :].astype(F32)

                    widen(span(1 - c, par, k))
                    self.feed(k).start()
                    widen(span(c, par, k))
                    if n_x > 1 and with_ring:
                        self.ring(k).start()
                    self.across(k, c).start()
                    widen(span(c, 1 - par, k))
                    self.again(k, c).start()

                for o in range(1, n_pp):
                    self.id_copy(o).start()

        def early_ring(self):
            @pl.when(mate == self.source)
            def _():
                @pl.loop(0, n_chunk)
                def _(k):
                    self.ring(k).wait_recv()
                    if n_x > 1:
                        self.ring(k).start()

        def late_ring(self, lo, hi):
            if n_x > 1:
                @pl.when(self.is_src)
                def _():
                    @pl.loop(lo, hi)
                    def _(k):
                        self.ring(k).start()

        def late_plane(self):
            @pl.when(mate == self.source)
            def _():
                @pl.loop(0, n_chunk)
                def _(k):
                    self.plane(k, par).start()

        def steps(self, lo, hi, early=False):
            @pl.when(jnp.logical_not(self.is_src))
            def _():
                @pl.loop(lo, hi)
                def _(k):
                    @pl.when(jnp.logical_and(k < n_chunk, jnp.logical_or(mate != self.source, not early)))
                    def _():
                        self.ring(k).wait_recv()
                        if n_x > 1:
                            @pl.when(self.dist < n_x - 1)
                            def _():
                                if early:
                                    @pl.when(jnp.logical_and(p == n_pp - 1, k >= 2))
                                    def _():
                                        self.ring(k - 2).wait_send()

                                self.ring(k).start()

                        self.plane(k, par).start()

                        @pl.when(mate != self.source)
                        def _():
                            self.across(k, c).start()

                    @pl.when(k >= lag)
                    def _():
                        self.plane(k - lag, 1 - par).wait_recv()

                        @pl.when(mate != self.source)
                        def _():
                            self.again(k - lag, c).start()

        def collect(self, g, parts):
            @pl.when(jnp.logical_not(self.is_src))
            def _():
                if g == 0:
                    self.id_copy(1).wait_recv()

                per_part, count = n_chunk // parts, tok // parts

                @pl.loop(g * per_part, (g + 1) * per_part)
                def _(k):
                    self.across(k, 1 - c).wait_recv()
                    self.again(k, 1 - c).wait_recv()

                tile = min(128, count)

                @pl.loop(0, count // tile)
                def _(k):
                    here = pl.ds(pl.multiple_of(g * count + k * tile, tile), tile)
                    self.low[here, :] = self.buf[here, :].astype(BF16)

        def settle(self):
            @pl.when(self.is_src)
            def _():
                for o in range(1, n_pp):
                    self.id_copy(o).wait_send()

            @pl.loop(0, n_chunk)
            def _(k):
                @pl.when(self.is_src)
                def _():
                    self.feed(k).wait_send()

                @pl.when(jnp.logical_not(self.is_src))
                def _():
                    self.plane(k, par).wait_send()

                if n_x > 1:
                    begun = n_chunk if self.a == 0 else n_chunk - 2

                    @pl.when(jnp.logical_and(self.dist < n_x - 1, jnp.logical_or(p != n_pp - 1, k >= begun)))
                    def _():
                        self.ring(k).wait_send()

                @pl.when(mate != self.source)
                def _():
                    self.across(k, c).wait_send()
                    self.again(k, c).wait_send()

    hid_in, dx_in = Stream(0), Stream(1)
    def logits(g):
        cols = pl.ds(g * wide, wide)
        h = hid_ref[cols, :]
        top = jnp.full((1, wide), LOW, F32)
        for d in range(n_dp):
            lg = lax.dot_general(tab_ref[d], h, (((1,), (1,)), ((), ())), preferred_element_type=F32)
            if d == n_dp - 1 and short < rows:
                ok = first_row(d) + lax.broadcasted_iota(jnp.int32, (rows, wide), 0) < vocab
                lg = jnp.where(ok, lg, LOW)
            exp_at(g, d)[...] = lg
            top = jnp.maximum(top, jnp.max(lg, axis=0, keepdims=True))
        tot = jnp.zeros((1, wide), F32)
        for d in range(n_dp):
            e = jnp.exp(exp_at(g, d)[...] - top)
            exp_at(g, d)[...] = e
            tot = tot + jnp.sum(e, axis=0, keepdims=True)
        stat_ref[0:1, cols] = top
        stat_ref[1:2, cols] = tot

    with scope("begin"):
        hid_in.begin(True)
        dx_in.begin(False)
        each_table_copy(lambda cp: cp.wait())
        for d in range(n_dp):
            tab_ref[d] = part_at(d, 0, 4)[...].astype(BF16)
    with scope("early"):
        dx_in.early_ring()
    dist = dx_in.dist

    def clip(value):
        return jnp.clip(jnp.where(p == 1, 0, value), 0, last)

    near = jnp.where(jnp.logical_or(jnp.logical_and(c == 0, dist == 1), jnp.logical_and(c == 1, dist >= 2)), 1, 0)
    near = jnp.where(jnp.logical_or(p == n_pp - 1, hid_in.dist == n_x - 1), 0, near)
    at_zero = near * jnp.where(c == 0, 2, jnp.maximum(12 - 3 * dist, 0))
    at_zero = jnp.minimum(at_zero, last - (n_piece - 2))
    at_half = at_zero + (n_piece - 2) * near
    at_one = jnp.where(p == n_pp - 1, last, jnp.where(c == 0, 11 - 3 * dist, 18 - 3 * dist))
    at_two = jnp.where(p == n_pp - 1, last, jnp.where(c == 0, at_one + 2, at_one + 3))
    at_one = jnp.maximum(clip(at_one), at_half)
    at_two = jnp.maximum(clip(at_two), at_one)
    at_three = jnp.maximum(jnp.minimum(at_two + jnp.where(p == 1, 0, n_dp), last), min(last, per_group + lag))
    at_four = jnp.maximum(at_three, min(last, max(n_chunk, 2 * per_group + lag)))

    def prepare(g):
        with scope(f"hid_collect{g}"):
            hid_in.collect(g, n_piece)
        with scope(f"logits{g}"):
            logits(g)

    at_end = jnp.logical_and(hid_in.dist == n_x - 1, jnp.logical_not(hid_in.is_src))
    pair = n_chunk // n_piece

    @pl.when(at_end)
    def _():
        lo = 0
        for g in range(n_piece - 2):
            hi = min(last, (g + 1) * pair + lag + 1)
            with scope(f"hid{g}"):
                hid_in.steps(lo, hi)
            prepare(g)
            lo = hi
        with scope("hid_end"):
            hid_in.steps(lo, last)
        dx_in.late_ring(0, n_chunk)
        dx_in.late_plane()

    @pl.when(jnp.logical_not(at_end))
    def _():
        with scope("hid_end"):
            hid_in.steps(0, n_chunk)
            dx_in.late_ring(0, 2)
            hid_in.steps(n_chunk, last)
            dx_in.late_ring(2, n_chunk)
            dx_in.late_plane()
        with scope("dx0"):
            dx_in.steps(0, at_zero, True)
        for g in range(n_piece - 2):
            prepare(g)
            dx_in.steps(at_zero + g * near, at_zero + (g + 1) * near, True)

    for g in range(n_piece - 2, n_piece):
        prepare(g)

    def swap(src, buf, send, recv, axis, me, n):
        return [remote(src, buf.at[o - 1], send.at[o - 1], recv.at[o - 1], {axis: lax.rem(me + o, n)}) for o in range(1, n)]

    def merge(src, buf, n):
        top = src[0:1, :]
        for o in range(1, n):
            top = jnp.maximum(top, buf[o - 1, 0:1, :])
        tot = src[1:2, :] * jnp.exp(src[0:1, :] - top)
        for o in range(1, n):
            tot = tot + buf[o - 1, 1:2, :] * jnp.exp(buf[o - 1, 0:1, :] - top)
        return top, tot

    def local_ids(ref, start, count):
        ids = ref[:, start:start + count] - z * vocab
        return jnp.where(ids < vocab, ids, -1)

    def row_ids(d, count):
        return first_row(d) + lax.broadcasted_iota(jnp.int32, (rows, count), 0)

    stage = swap(stat_ref, buf_p, sp_s, sp_r, "pp", p, n_pp)
    for cp in stage:
        cp.start()
    with scope("dx1"):
        if n_x > 1:
            @pl.when(p == n_pp - 1)
            def _():
                @pl.loop(0, n_chunk)
                def _(k):
                    hid_in.ring(k).wait_send()

        dx_in.steps(at_half, at_one, True)
    with scope("stat1"):
        for cp in stage:
            cp.wait()
    top, tot = merge(stat_ref, buf_p, n_pp)
    mid_ref[0:1, :] = top
    mid_ref[1:2, :] = tot
    stage = swap(mid_ref, buf_z, sz_s, sz_r, "tp", z, n_tp)
    for cp in stage:
        cp.start()
    with scope("dx2"):
        dx_in.steps(at_one, at_two, True)
    with scope("stat2"):
        for cp in stage:
            cp.wait()
    top, tot = merge(mid_ref, buf_z, n_tp)
    mid_ref[0:1, :] = jnp.exp(stat_ref[0:1, :] - top) / (tot * tok)

    def head(d):
        for g in range(0, n_piece, per_band):
            count = min(per_band, n_piece - g)
            cols = pl.ds(g * wide, count * wide)
            prob = big_ref[pl.ds(pl.multiple_of(exp_row + (g // per_band) * n_dp * rows + d * rows, 8), rows), pl.ds(0, count * wide)] * mid_ref[0:1, cols]
            hit = local_ids(lab_ref, g * wide, count * wide) == row_ids(d, count * wide)
            dl_ref[:, cols] = jnp.where(hit, prob - 1.0 / tok, prob).astype(BF16)
        for q in range(4):
            part_at(d, q)[...] = jnp.dot(dl_ref[...], hid_ref[:, q * dq:(q + 1) * dq], preferred_element_type=F32)

    def lookup(g):
        def add(d):
            hot = (local_ids(look_ref, g * group, group) == row_ids(d, group)).astype(BF16)
            dl_ref[:, 0:group] = hot
            for q in range(4):
                part_at(d, q)[...] += jnp.dot(dl_ref[:, 0:group], dx_ref[g * group:(g + 1) * group, q * dq:(q + 1) * dq], preferred_element_type=F32)
        return add

    with scope("head"):
        @pl.loop(0, n_dp)
        def _(d):
            head(d)
            dx_in.steps(jnp.minimum(at_two + d, at_three), jnp.minimum(at_two + d + 1, at_three), True)

        dx_in.steps(jnp.minimum(at_two + n_dp, at_three), at_three, True)
    with scope("dx_group0"):
        dx_in.collect(0, n_group)
        pl.loop(0, n_dp)(lookup(0))
    with scope("dx4"):
        dx_in.steps(at_three, at_four, True)
    with scope("dx_group1"):
        dx_in.collect(1, n_group)
        pl.loop(0, n_dp)(lookup(1))
    with scope("dx5"):
        dx_in.steps(at_four, last, True)
    with scope("dx_group2"):
        dx_in.collect(2, n_group)

    far = lax.rem(y + 2, n_dp)

    def reduce_copy(i, d, half, row, where):
        return remote(part_at(d, 2 * half, 2), half_at(row, half), rs_s.at[i], rs_r.at[i], {"dp": where})

    rel_a = reduce_copy(0, far, 0, rel_row, up_y)
    rel_b = reduce_copy(1, far, 1, rel_row, down_y)
    one_b = reduce_copy(2, up_y, 1, one_row, up_y)
    one_a = reduce_copy(3, down_y, 0, one_row, down_y)
    com_a = reduce_copy(4, up_y, 0, com_row, up_y)
    com_b = reduce_copy(5, down_y, 1, com_row, down_y)
    add = lookup(n_group - 1)
    add(far)
    rel_a.start()
    rel_b.start()
    add(up_y)
    one_b.start()
    add(down_y)
    one_a.start()
    add(y)
    hid_in.settle()
    dx_in.settle()

    def moments(lo, hi, sem):
        return pltpu.make_async_copy(sq_ref.at[pl.ds(lo, hi - lo)], big_ref.at[pl.ds(lo, hi - lo)], pre_s.at[sem])

    loads = [moments(0, min(part_row, vocab), 0)]
    loads[0].start()
    with scope("relay"):
        rel_a.wait_recv()
    part_at(up_y, 0, 2)[...] += half_at(rel_row, 0)[...]
    com_a.start()
    rel_b.wait_recv()
    part_at(down_y, 2, 2)[...] += half_at(rel_row, 1)[...]
    com_b.start()
    own = y * n_pp + p
    square = jnp.zeros((8, 128), F32)
    with scope("one"):
        one_a.wait_recv()
        one_b.wait_recv()
    for half, cp in ((0, com_a), (1, com_b)):
        with scope("com"):
            cp.wait_recv()
        for q in range(2):
            cols = pl.ds((2 * half + q) * dq, dq)
            total = (part_at(y, 2 * half + q)[...] + big_ref[pl.ds(com_row, rows), cols] + big_ref[pl.ds(one_row, rows), cols]) * (1.0 / n_dp)
            g_ref[own, 2 * half + q] = total
            lanes = jnp.sum((total * total).reshape(rows // 8, 8, dq), axis=0)
            for i in range(0, dq, 128):
                square = square + lanes[:, i:i + 128]

    def block(xx, yy):
        return lax.rem(yy + 2 * n_dp, n_dp) * n_pp + 2 * lax.rem(xx + 2 * n_x, n_x) + c

    colours = []
    for q, (axes, sign) in enumerate((("xy", 1), ("xy", -1), ("yx", 1), ("yx", -1))):
        sizes = (n_x, n_dp) if axes == "xy" else (n_dp, n_x)
        to_x = {"pp": 2 * lax.rem(x + sign + n_x, n_x) + c}
        to_y = {"dp": lax.rem(y + sign + n_dp, n_dp)}
        dest = (to_x, to_y) if axes == "xy" else (to_y, to_x)
        colours.append((q, axes, sign, sizes, dest, ring_plan(*sizes)))

    def holder(axes, sign, s, t):
        return block(x - sign * s, y - sign * t) if axes == "xy" else block(x - sign * t, y - sign * s)

    def message(colour, item, coming):
        q, axes, sign, _, dest, plan = colour
        phase, s, t = item
        at = plan.index(item)
        s_at, t_at = (s + coming, t) if phase == 1 else (s, t + coming)
        b = holder(axes, sign, s_at, t_at)
        return remote(g_ref.at[b, q], g_ref.at[b, q], ag_s.at[q, at], ag_r.at[q, at], dest[phase - 1])

    def mate_copy(q, slot, b):
        return remote(g_ref.at[b, q], g_ref.at[b, q], d_s.at[q, slot], d_r.at[q, slot], {"pp": mate})

    sends = []

    def push(cp):
        cp.start()
        sends.append(cp)

    for colour in colours:
        if colour[3][0] > 1:
            push(message(colour, (1, 0, 0), 0))
    for colour in colours:
        if colour[3][1] > 1:
            push(message(colour, (2, 0, 0), 0))

    def norm_swap(value, buf, send, recv, axis, me, n):
        buf[me] = value
        return [remote(buf.at[me], buf.at[me], send.at[o - 1], recv.at[o - 1], {axis: lax.rem(me + o, n)}) for o in range(1, n)], [
            remote(buf.at[lax.rem(me + n - o, n)], buf.at[lax.rem(me + n - o, n)], send.at[o - 1], recv.at[o - 1], {axis: lax.rem(me + o, n)}) for o in range(1, n)]

    norm_out, norm_in = norm_swap(square, nb_p, np_s, np_r, "pp", p, n_pp)
    for cp in norm_out:
        push(cp)
    for q in range(4):
        push(mate_copy(q, 0, own))

    for cp in (rel_a, rel_b, one_a, one_b, com_a, com_b):
        cp.wait_send()
    if part_row < vocab:
        loads.append(moments(part_row, vocab, 1))
        loads[1].start()

    steps = n_x * n_dp - 1
    for i in range(steps):
        for colour in colours:
            q, axes, sign, sizes, dest, plan = colour
            phase, s, t = plan[i]
            message(colour, plan[i], 1).wait_recv()
            if phase == 1:
                if s + 1 < sizes[0] - 1:
                    push(message(colour, (1, s + 1, 0), 0))
                if sizes[1] > 1:
                    push(message(colour, (2, s + 1, 0), 0))
                push(mate_copy(q, i + 1, holder(axes, sign, s + 1, 0)))
            else:
                if t + 1 < sizes[1] - 1:
                    push(message(colour, (2, s, t + 1), 0))
                push(mate_copy(q, i + 1, holder(axes, sign, s, t + 1)))
        if i == 0:
            for cp in norm_in:
                cp.wait_recv()
            total = nb_p[0]
            for o in range(1, n_pp):
                total = total + nb_p[o]
            norm_out, norm_in = norm_swap(total, nb_y, ny_s, ny_r, "dp", y, n_dp)
            for cp in norm_out:
                push(cp)
        if i == 1:
            for cp in norm_in:
                cp.wait_recv()
            total = nb_y[0]
            for o in range(1, n_dp):
                total = total + nb_y[o]
            norm_out, norm_in = norm_swap(total, nb_z, nz_s, nz_r, "tp", z, n_tp)
            for cp in norm_out:
                push(cp)
        if i == 2:
            for cp in norm_in:
                cp.wait_recv()
            total = nb_z[0]
            for o in range(1, n_tp):
                total = total + nb_z[o]
            norm = jnp.sqrt(jnp.sum(total, axis=(0, 1), keepdims=True))
            scale_ref[...] = jnp.broadcast_to(CLIP_NORM / jnp.maximum(norm, CLIP_NORM), (8, 128))

    for q, axes, sign, sizes, dest, plan in colours:
        for i in range(steps + 1):
            if i == 0:
                b = own
            else:
                phase, s, t = plan[i - 1]
                b = holder(axes, sign, s + 1, 0) if phase == 1 else holder(axes, sign, s, t + 1)
            mate_copy(q, i, b + 1 - 2 * c).wait_recv()
    for cp in sends:
        cp.wait_send()
    for cp in loads:
        cp.wait()


def plane_gradient(master, acts, ids, exp_avg_sq, n_tp, n_dp, n_pp):
    vocab, dim = master.shape
    tok = acts.shape[0]
    rows = -(-vocab // (n_pp * n_dp))
    rows = -(-rows // 8) * 8
    dq = dim // 4
    n_chunk = 12 if tok % (4 * 12 * 8) == 0 else 6
    lag = 2
    steps = (n_pp // 2) * n_dp
    per_band = min(6, dim // (tok // 6))
    big = max(n_dp * n_pp * rows, 2 * tok + (-(-6 // per_band) * n_dp + n_dp + 3) * rows)
    full = pl.BlockSpec(memory_space=VMEM)
    any_space = pl.BlockSpec(memory_space=pl.ANY)
    chunk = DMA((2, n_chunk))
    return pl.pallas_call(
        functools.partial(grad_kernel, n_tp, n_dp, n_pp, n_chunk, lag),
        out_shape=(VMEM((n_dp * n_pp, 4, rows, dq), F32), jax.ShapeDtypeStruct((8, 128), F32), VMEM((big, dim), F32)),
        in_specs=[any_space, any_space, full, any_space],
        out_specs=(full, full, full),
        scratch_shapes=[
            VMEM((tok, dim), BF16), VMEM((tok, dim), BF16),
            VMEM((1, tok), jnp.int32), VMEM((1, tok), jnp.int32), VMEM((n_dp, rows, dim), BF16), VMEM((rows, tok), BF16),
            VMEM((2, tok), F32), VMEM((2, tok), F32), VMEM((n_pp - 1, 2, tok), F32), VMEM((n_tp - 1, 2, tok), F32),
            VMEM((n_pp, 8, 128), F32), VMEM((n_dp, 8, 128), F32), VMEM((n_tp, 8, 128), F32),
            DMA((1 + n_dp,)), *[chunk] * 9, DMA((2, n_pp - 1)), DMA((2,)),
            DMA((n_pp - 1,)), DMA((n_pp - 1,)), DMA((n_tp - 1,)), DMA((n_tp - 1,)), DMA((6,)), DMA((6,)),
            DMA((n_pp - 1,)), DMA((n_pp - 1,)), DMA((n_dp - 1,)), DMA((n_dp - 1,)), DMA((n_tp - 1,)), DMA((n_tp - 1,)),
            DMA((4, steps)), DMA((4, steps)), DMA((4, steps)), DMA((4, steps)), DMA((2,)),
        ],
        compiler_params=pltpu.CompilerParams(collective_id=0, has_side_effects=True, vmem_limit_bytes=SMALL_GRANT),
        name="plane_gradient",
    )(master, acts, ids, exp_avg_sq)


def adamw_kernel(n_slot, ahead, tile, scale_ref, g_ref, v_ref, e_hbm, m_hbm, ne_hbm, nm_hbm, nv_hbm, nb_hbm, e_buf, m_buf, v_buf, b_buf, in_s, out_s):
    rows, dq = g_ref.shape[2:]
    per_block, per_tile = rows // 8, tile // 8
    n_tile = e_hbm.shape[0] // tile
    scale = scale_ref[0:1, 0:1]

    def span(i):
        return pl.ds(pl.multiple_of(i * tile, 8), tile)

    def loads(i):
        slot = lax.rem(i, n_slot)
        return [pltpu.make_async_copy(hbm.at[span(i)], buf.at[slot], in_s.at[a, slot]) for a, (hbm, buf) in enumerate(((e_hbm, e_buf), (m_hbm, m_buf)))]

    def stores(i):
        slot = lax.rem(i, n_slot)
        return [pltpu.make_async_copy(buf.at[slot], hbm.at[span(i)], out_s.at[a, slot]) for a, (buf, hbm) in enumerate(((e_buf, ne_hbm), (m_buf, nm_hbm), (v_buf, nv_hbm), (b_buf, nb_hbm)))]

    for i in range(min(ahead, n_tile)):
        for cp in loads(i):
            cp.start()

    @pl.loop(0, n_tile)
    def _(i):
        slot = lax.rem(i, n_slot)

        @pl.when(i + ahead < n_tile)
        def _():
            @pl.when(i + ahead >= n_slot)
            def _():
                for cp in stores(i + ahead - n_slot):
                    cp.wait()

            for cp in loads(i + ahead):
                cp.start()

        for cp in loads(i):
            cp.wait()
        for r in range(per_tile):
            group = i * per_tile + r
            blk = group // per_block
            inside = pl.ds(pl.multiple_of((group - blk * per_block) * 8, 8), 8)
            at = pl.ds(8 * r, 8)
            for q in range(4):
                cols = pl.ds(q * dq, dq)
                g = g_ref[blk, q, inside, :] * scale
                e = e_buf[slot, at, cols]
                m = BETA_ONE * m_buf[slot, at, cols] + (1.0 - BETA_ONE) * g
                v = BETA_TWO * v_ref[pl.ds(pl.multiple_of(group * 8, 8), 8), cols] + (1.0 - BETA_TWO) * g * g
                step = (m * (1.0 / (1.0 - BETA_ONE ** OPT_STEP))) / (jnp.sqrt(v * (1.0 / (1.0 - BETA_TWO ** OPT_STEP))) + ADAM_EPS)
                ne = e - LEARN_RATE * (step + WEIGHT_DECAY * e)
                e_buf[slot, at, cols] = ne
                m_buf[slot, at, cols] = m
                v_buf[slot, at, cols] = v
                b_buf[slot, at, cols] = ne.astype(BF16)
        for cp in stores(i):
            cp.start()

    for i in range(max(0, n_tile - n_slot), n_tile):
        for cp in stores(i):
            cp.wait()


def adamw(scale, grad, second, master, exp_avg):
    vocab, dim = master.shape
    tile = next(t for t in (48, 32, 16, 8) if vocab % t == 0)
    n_slot = 14
    full = pl.BlockSpec(memory_space=VMEM)
    any_space = pl.BlockSpec(memory_space=pl.ANY)
    f32 = jax.ShapeDtypeStruct((vocab, dim), F32)
    count = vocab * dim
    ring = VMEM((n_slot, tile, dim), F32)
    return pl.pallas_call(
        functools.partial(adamw_kernel, n_slot, 8, tile),
        out_shape=(f32, f32, f32, jax.ShapeDtypeStruct((vocab, dim), BF16)),
        in_specs=[full, full, full, any_space, any_space],
        out_specs=(any_space,) * 4,
        scratch_shapes=[ring, ring, ring, VMEM((n_slot, tile, dim), BF16), DMA((2, n_slot)), DMA((4, n_slot))],
        cost_estimate=pl.CostEstimate(flops=20 * count, bytes_accessed=22 * count, transcendentals=2 * count),
        compiler_params=pltpu.CompilerParams(vmem_limit_bytes=SMALL_GRANT),
        name="adamw",
    )(scale, in_vmem(grad), in_vmem(second), master, exp_avg)


def solution(mesh):
    n_pp, n_dp, n_tp = mesh.shape["pp"], mesh.shape["dp"], mesh.shape["tp"]
    table_spec = P("tp", None)

    def device_step(master, exp_avg, exp_avg_sq, stage_ids, stage_acts):
        vocab, dim = master.shape
        tok = stage_ids.shape[1] * stage_ids.shape[2]
        acts = stage_acts.reshape(tok, dim)
        grad, scale, second = plane_gradient(master, acts, stage_ids.reshape(1, tok), exp_avg_sq, n_tp, n_dp, n_pp)
        return adamw(scale, grad, second, master, exp_avg)

    return jax.shard_map(device_step, mesh=mesh, in_specs=(table_spec, table_spec, table_spec, P("pp", "dp", None), P("pp", "dp", None, None)), out_specs=(table_spec, table_spec, table_spec, table_spec), check_vma=False)
```

profile of v0, /device:TPU:1, one launch (start us, length us, event | category | flops | bytes accessed | tf_op | source)
XLA Modules:
  0.0 234.3 jit_solution(17036819489539183203)
XLA Ops:
  0.6 185.6 %plane_gradient.1 = (f32[32,4,200,256]{3,2,1,0:T(8,128)S(1)}, f32[8,128]{1,0:T(8,128)}, f32[6400,1024]{1,0:T(8,128)S(1)}) custom-call(f32[6288,1024]{1,0:T(8,128)} %e_hbm.1, bf16[1536,1024]{1,0:T(8,128)(2,1)} %bitcast.2, s32[1,1536]{1,0:T(1,128)} %bitcast.3, f32[6288,1024]{1,0:T(8,128)} %sq_ref.1), custom_call_target="tpu_custom_call" | custom-call | tf_op jit(solution)/shard_map/plane_gradient/pallas_call | solution.py:615
  186.2 47.9 %adamw.1 = (f32[6288,1024]{1,0:T(8,128)}, f32[6288,1024]{1,0:T(8,128)}, f32[6288,1024]{1,0:T(8,128)}, bf16[6288,1024]{1,0:T(8,128)(2,1)}) custom-call(f32[8,128]{1,0:T(8,128)} %get-tuple-element.7.scale_ref, f32[32,4,200,256]{3,2,1,0:T(8,128)S(1)} %get-tuple-element.8.g_ref, f32[6400,1024]{1,0:T(8,128)S(1)} %get-tuple-element.9.v_ref, f32[6288,1024]{1,0:T(8,128)} %e_hbm.1, ...), custom_call_target="tpu_custom_call" | custom-call | flops 128778240 | bytes 141656064 | tf_op jit(solution)/shard_map/adamw/pallas_call | solution.py:706
where the time goes:
time: 235 us; the launch traced here: 234 us
  Pallas kernels  234 us (100%)
    pallas_call x1, Pallas kernels, plane_gradient(): pl.pallas_call(functools.partial(grad_kernel, n_tp, n_dp, n_pp, n_chunk,...  186 us
    pallas_call x1, Pallas kernels, adamw(): pl.pallas_call(functools.partial(adamw_kernel, n_slot, 8, tile), out_shap...  47.9 us

commit v1 on v0

--- a/solution.py
+++ b/solution.py
@@ -115,6 +115,9 @@
             self.is_src = p == self.source
             s_x = self.source // 2
             self.dist = lax.rem(jnp.where(c == 0, x - s_x, s_x - x) + n_x, n_x)
+            self.cut = a == 1 and n_x > 2
+            ends = jnp.where(c == 0, n_x - 2, n_x - 1) if self.cut else n_x - 1
+            self.passes = self.dist < ends
 
         def hop(self, part, send, recv, where):
             return remote(self.buf.at[part], self.buf.at[part], send, recv, where)
@@ -124,6 +127,9 @@
 
         def ring(self, k):
             return self.hop(span(c, par, k), send_x.at[self.a, k], recv_x.at[self.a, k], {"pp": next_p})
+
+        def direct(self, k):
+            return self.hop(span(c, par, k), send_z.at[self.a, k], recv_x.at[self.a, k], {"pp": lax.rem(p + n_pp - 2, n_pp)})
 
         def plane(self, k, parity):
             return self.hop(span(c, parity, k), send_z.at[self.a, k], recv_z.at[self.a, k], {"tp": next_z})
@@ -176,6 +182,8 @@
                     @pl.loop(lo, hi)
                     def _(k):
                         self.ring(k).start()
+                        if self.cut:
+                            self.direct(k).start()
 
         def late_plane(self):
             @pl.when(mate == self.source)
@@ -193,7 +201,7 @@
                     def _():
                         self.ring(k).wait_recv()
                         if n_x > 1:
-                            @pl.when(self.dist < n_x - 1)
+                            @pl.when(self.passes)
                             def _():
                                 if early:
                                     @pl.when(jnp.logical_and(p == n_pp - 1, k >= 2))
@@ -247,6 +255,8 @@
                 @pl.when(self.is_src)
                 def _():
                     self.feed(k).wait_send()
+                    if self.cut:
+                        self.direct(k).wait_send()
 
                 @pl.when(jnp.logical_not(self.is_src))
                 def _():
@@ -255,7 +265,7 @@
                 if n_x > 1:
                     begun = n_chunk if self.a == 0 else n_chunk - 2
 
-                    @pl.when(jnp.logical_and(self.dist < n_x - 1, jnp.logical_or(p != n_pp - 1, k >= begun)))
+                    @pl.when(jnp.logical_and(self.passes, jnp.logical_or(p != n_pp - 1, k >= begun)))
                     def _():
                         self.ring(k).wait_send()
 
@@ -292,12 +302,12 @@
             tab_ref[d] = part_at(d, 0, 4)[...].astype(BF16)
     with scope("early"):
         dx_in.early_ring()
-    dist = dx_in.dist
+    dist = jnp.where(jnp.logical_and(c == 0, dx_in.dist == n_x - 1), 1, dx_in.dist)
 
     def clip(value):
         return jnp.clip(jnp.where(p == 1, 0, value), 0, last)
 
-    near = jnp.where(jnp.logical_or(jnp.logical_and(c == 0, dist == 1), jnp.logical_and(c == 1, dist >= 2)), 1, 0)
+    near = jnp.where(jnp.logical_or(jnp.logical_and(c == 0, dx_in.dist == 1), jnp.logical_and(c == 1, dist >= 2)), 1, 0)
     near = jnp.where(jnp.logical_or(p == n_pp - 1, hid_in.dist == n_x - 1), 0, near)
     at_zero = near * jnp.where(c == 0, 2, jnp.maximum(12 - 3 * dist, 0))
     at_zero = jnp.minimum(at_zero, last - (n_piece - 2))

time: 235 us -> 228 us (0.970)
  Pallas kernels: 234 us -> 226 us
    pallas_call x1, Pallas kernels: 186 us -> 178 us  [plane_gradient(): pl.pallas_call(functools.partial(grad_kernel, n_tp, n_dp, n_pp, n_chunk,...]
where the time goes in v1:
time: 228 us; the launch traced here: 227 us
  Pallas kernels  226 us (99%)
    pallas_call x1, Pallas kernels, plane_gradient(): pl.pallas_call(functools.partial(grad_kernel, n_tp, n_dp, n_pp, n_chunk,...  178 us
    pallas_call x1, Pallas kernels, adamw(): pl.pallas_call(functools.partial(adamw_kernel, n_slot, 8, tile), out_shap...  47.9 us

profile of v1, /device:TPU:1, one launch (start us, length us, event | category | flops | bytes accessed | tf_op | source)
XLA Modules:
  0.0 226.9 jit_solution(9672638336927174765)
XLA Ops:
  0.6 178.1 %plane_gradient.1 = (f32[32,4,200,256]{3,2,1,0:T(8,128)S(1)}, f32[8,128]{1,0:T(8,128)}, f32[6400,1024]{1,0:T(8,128)S(1)}) custom-call(f32[6288,1024]{1,0:T(8,128)} %e_hbm.1, bf16[1536,1024]{1,0:T(8,128)(2,1)} %bitcast.2, s32[1,1536]{1,0:T(1,128)} %bitcast.3, f32[6288,1024]{1,0:T(8,128)} %sq_ref.1), custom_call_target="tpu_custom_call" | custom-call | tf_op jit(solution)/shard_map/plane_gradient/pallas_call | solution.py:625
  178.8 47.9 %adamw.1 = (f32[6288,1024]{1,0:T(8,128)}, f32[6288,1024]{1,0:T(8,128)}, f32[6288,1024]{1,0:T(8,128)}, bf16[6288,1024]{1,0:T(8,128)(2,1)}) custom-call(f32[8,128]{1,0:T(8,128)} %get-tuple-element.7.scale_ref, f32[32,4,200,256]{3,2,1,0:T(8,128)S(1)} %get-tuple-element.8.g_ref, f32[6400,1024]{1,0:T(8,128)S(1)} %get-tuple-element.9.v_ref, f32[6288,1024]{1,0:T(8,128)} %e_hbm.1, ...), custom_call_target="tpu_custom_call" | custom-call | flops 128778240 | bytes 141656064 | tf_op jit(solution)/shard_map/adamw/pallas_call | solution.py:716

commit v2 on v1

--- a/solution.py
+++ b/solution.py
@@ -346,9 +346,8 @@
     def _():
         with scope("hid_end"):
             hid_in.steps(0, n_chunk)
-            dx_in.late_ring(0, 2)
+            dx_in.late_ring(0, n_chunk)
             hid_in.steps(n_chunk, last)
-            dx_in.late_ring(2, n_chunk)
             dx_in.late_plane()
         with scope("dx0"):
             dx_in.steps(0, at_zero, True)

time: 228 us -> 228 us (level)
  no operation moved by 1% of the time
where the time goes in v2:
time: 228 us; the launch traced here: 227 us
  Pallas kernels  226 us (99%)
    pallas_call x1, Pallas kernels, plane_gradient(): pl.pallas_call(functools.partial(grad_kernel, n_tp, n_dp, n_pp, n_chunk,...  178 us
    pallas_call x1, Pallas kernels, adamw(): pl.pallas_call(functools.partial(adamw_kernel, n_slot, 8, tile), out_shap...  47.9 us

profile of v2, /device:TPU:1, one launch (start us, length us, event | category | flops | bytes accessed | tf_op | source)
XLA Modules:
  0.0 226.9 jit_solution(17480380848862058041)
XLA Ops:
  0.6 178.1 %plane_gradient.1 = (f32[32,4,200,256]{3,2,1,0:T(8,128)S(1)}, f32[8,128]{1,0:T(8,128)}, f32[6400,1024]{1,0:T(8,128)S(1)}) custom-call(f32[6288,1024]{1,0:T(8,128)} %e_hbm.1, bf16[1536,1024]{1,0:T(8,128)(2,1)} %bitcast.2, s32[1,1536]{1,0:T(1,128)} %bitcast.3, f32[6288,1024]{1,0:T(8,128)} %sq_ref.1), custom_call_target="tpu_custom_call" | custom-call | tf_op jit(solution)/shard_map/plane_gradient/pallas_call | solution.py:624
  178.8 47.9 %adamw.1 = (f32[6288,1024]{1,0:T(8,128)}, f32[6288,1024]{1,0:T(8,128)}, f32[6288,1024]{1,0:T(8,128)}, bf16[6288,1024]{1,0:T(8,128)(2,1)}) custom-call(f32[8,128]{1,0:T(8,128)} %get-tuple-element.7.scale_ref, f32[32,4,200,256]{3,2,1,0:T(8,128)S(1)} %get-tuple-element.8.g_ref, f32[6400,1024]{1,0:T(8,128)S(1)} %get-tuple-element.9.v_ref, f32[6288,1024]{1,0:T(8,128)} %e_hbm.1, ...), custom_call_target="tpu_custom_call" | custom-call | flops 128778240 | bytes 141656064 | tf_op jit(solution)/shard_map/adamw/pallas_call | solution.py:715
